TPU v7x, 256 devices: a whole 4x4x8 slice. The times are simulated.
256 devices in a mesh: dp: 16 (over z_lo, y), mp: 16 (over x, z_hi, core).
Axes of the slice: x: 4, y: 4, z: 8 (z_hi: 2, z_lo: 4; z = z_hi * 4 + z_lo), core: 2. Of those that a mesh axis runs over, the one named last changes fastest.
Arguments:
- image_tokens: bfloat16 [16, 192, 3072], P('dp'), may hold values from -6 to 6
- text_tokens: bfloat16 [16, 64, 3072], P('dp'), may hold values from -6 to 6
- null_prompt: bfloat16 [64, 3072], replicated, may hold values from -6 to 6
- drop_flags: int32 [16], P('dp'), may hold values 0 or 1
- time_index: int32 [16], P('dp'), may hold values from 0 to 31
- modulation: float32 [32, 3, 3072], replicated, may hold values from -3 to 3
- w_up: bfloat16 [3072, 12288], P('dp', 'mp'), may hold values from -0.109375 to 0.109375
- w_down: bfloat16 [12288, 3072], P('mp', 'dp'), may hold values from -0.0546875 to 0.0546875
- d_output: bfloat16 [16, 256, 3072], P('dp'), may hold values from -6 to 6
Outputs:
- block_out: bfloat16 [16, 256, 3072], P('dp')
- d_tokens: bfloat16 [16, 256, 3072], P('dp')
- grad_up: float32 [3072, 12288], P('dp', 'mp')
- grad_down: float32 [12288, 3072], P('mp', 'dp')
- grad_null: float32 [64, 3072], replicated
All inputs are finite; a program needn't handle non-finite values. No bound on the sum of `drop_flags` on one device may be relied on, other than what follows from the above.
Results may differ from a plain program's by a relative error of at most 0.017.
Values may be sent and summed in bfloat16 or wider, within the bound.
A program may use at most 128 MiB of HBM per device.

v0:
```python
import functools

import jax
import jax.numpy as jnp
from jax import lax
from jax.experimental import pallas as pl
from jax.experimental.pallas import tpu as pltpu
from jax.sharding import Mesh
from jax.sharding import PartitionSpec as P

AXES = ("zl", "y", "x", "zh", "c")
MP = ("x", "zh", "c")
DP = ("zl", "y")
EPS = 1e-06
MESH = pl.DeviceIdType.MESH
BF = jnp.bfloat16
F32 = jnp.float32


def gelu_tanh(values):
    return jax.nn.gelu(values, approximate=True)


def remote(src, dst, ss, rs, **dev):
    return pltpu.make_async_remote_copy(
        src_ref=src, dst_ref=dst, send_sem=ss, recv_sem=rs, device_id=dev, device_id_type=MESH
    )


def meet(devices):
    barrier = pltpu.get_barrier_semaphore()
    for dev in devices:
        pl.semaphore_signal(barrier, inc=1, device_id=dev, device_id_type=MESH)
    pl.semaphore_wait(barrier, len(devices))


def along_z(zl, zh, dist):
    to = lax.rem(zh * 4 + zl + dist % 8, 8)
    return {"zl": lax.rem(to, 4), "zh": to // 4}


def gather_kernel(pk, ab, g, t, lsem, ws, wr, zs, zr, ys, yr, ps, pr, xs, xr, bs, br):
    zl, y, x, zh, c = (lax.axis_index(n) for n in AXES)
    meet(
        [{"y": lax.rem(y + d, 4)} for d in (1, 2, 3)]
        + [{"x": lax.rem(x + d, 4)} for d in (1, 3)]
        + [along_z(zl, zh, d) for d in (1, -1)]
        + [{"c": 1 - c}]
    )
    yp, yo, ym = lax.rem(y + 1, 4), lax.rem(y + 2, 4), lax.rem(y + 3, 4)
    xp, xm = lax.rem(x + 1, 4), lax.rem(x + 3, 4)
    qrt = ab.shape[1] // 4
    half = qrt // 2
    par = lax.rem(x, 2)
    peers = (ym, yp, yo)
    sent = []

    def rows(quarter, h, n=1):
        return pl.ds(pl.multiple_of(quarter * qrt + h * half, half), n * half)

    own_q = par * 2 + c
    x_q = (1 - par) * 2 + c
    sib_q = (par * 2 + (1 - c), (1 - par) * 2 + (1 - c))

    def w1(d):
        to = lax.rem(y + d, 4)
        return remote(pk.at[to], g.at[zl, y], ws.at[d - 1], wr.at[d - 1], y=to)

    for d in (1, 3, 2):
        w1(d).start()
        sent.append((None, w1(d)))
    locs = [pltpu.make_async_copy(pk.at[y], g.at[zl, y], lsem.at[0])]
    locs += [pltpu.make_async_copy(ab.at[a], t.at[a, y], lsem.at[1 + a]) for a in range(2)]
    for cp in locs:
        cp.start()

    for a in range(2):
        for way, to in ((0, yp), (1, ym)):
            cp = remote(
                ab.at[a, rows(own_q, 0, 2)],
                t.at[a, y, rows(own_q, 0, 2)],
                ys.at[a, way],
                yr.at[a, way],
                y=to,
            )
            cp.start()
            sent.append((None, cp))

    def zcopy(way, s, d):
        yd = lax.rem(y + 4 - d, 4)
        block = zl - s if way == 0 else zl + s
        src = pk.at[y] if (s == 0 and d == 0) else g.at[block, yd]
        to = zl + 1 if way == 0 else zl - 1
        return remote(src, g.at[block, yd], zs.at[way, s, d], zr.at[way, s, d], zl=to)

    def zsend(way, s, d):
        ok = (zl < 3) & (zl >= s) if way == 0 else (zl > 0) & (zl + s <= 3)

        @pl.when(ok)
        def _():
            zcopy(way, s, d).start()

        sent.append((ok, (way, s, d)))

    def ztick(s, d):
        for way in (0, 1):
            got = zl >= s if way == 0 else zl + s <= 3
            yd = lax.rem(y + 4 - d, 4)

            @pl.when(got)
            def _():
                block = zl - s if way == 0 else zl + s
                remote(
                    g.at[block, yd], g.at[block, yd], zs.at[way, s - 1, d], zr.at[way, s - 1, d], zl=zl
                ).wait_recv()

            if s <= 2:
                zsend(way, s, d)

    def wstep(d):
        if d:
            w1(d).wait_recv()
        for way in (0, 1):
            zsend(way, 0, d)

    wstep(0)
    wstep(1)
    wstep(3)

    def send_on(a, peer, h):
        src = t.at[a, peers[peer], rows(own_q, h)]
        for cp in (
            remote(src, src, xs.at[a, peer, h], xr.at[a, peer, h], x=(xp, xm)[h]),
            remote(src, src, bs.at[a, peer, h], br.at[a, peer, h], c=1 - c),
        ):
            cp.start()
            sent.append((None, cp))

    def direct(a, way):
        whole = t.at[a, peers[way], rows(own_q, 0, 2)]
        remote(whole, whole, ys.at[a, way], yr.at[a, way], y=y).wait_recv()
        part = t.at[a, peers[way], rows(own_q, way)]
        cp = remote(part, part, ps.at[a, way], pr.at[a, way], y=(yp, ym)[way])
        cp.start()
        sent.append((None, cp))
        for h in (0, 1):
            send_on(a, way, h)

    def relayed(a, h):
        part = t.at[a, yo, rows(own_q, h)]
        remote(part, part, ps.at[a, h], pr.at[a, h], y=y).wait_recv()
        send_on(a, 2, h)

    def from_x(a, peer):
        for h in (0, 1):
            part = t.at[a, peers[peer], rows(x_q, h)]
            remote(part, part, xs.at[a, peer, h], xr.at[a, peer, h], x=x).wait_recv()
            cp = remote(part, part, bs.at[a, peer, 2 + h], br.at[a, peer, 2 + h], c=1 - c)
            cp.start()
            sent.append((None, cp))

    ztick(1, 0)
    wstep(2)
    ztick(1, 1)
    direct(0, 1)
    ztick(1, 3)
    ztick(1, 2)
    direct(0, 0)
    ztick(2, 0)
    direct(1, 1)
    ztick(2, 1)
    relayed(0, 1)
    from_x(0, 1)
    direct(1, 0)
    ztick(2, 3)
    from_x(0, 0)
    ztick(2, 2)
    relayed(1, 1)
    relayed(0, 0)
    ztick(3, 0)
    from_x(1, 1)
    relayed(1, 0)
    ztick(3, 1)
    from_x(1, 0)
    from_x(0, 2)
    ztick(3, 3)
    ztick(3, 2)
    from_x(1, 2)
    for a in range(2):
        for peer in range(3):
            for kind in range(4):
                part = t.at[a, peers[peer], rows(sib_q[kind // 2], kind % 2)]
                remote(part, part, bs.at[a, peer, kind], br.at[a, peer, kind], c=c).wait_recv()
    for cp in locs:
        cp.wait()
    for ok, cp in sent:
        if ok is None:
            cp.wait_send()
        else:
            way, s, d = cp

            @pl.when(ok)
            def _():
                zcopy(way, s, d).wait_send()


def gather(pk, ab):
    n_tok, width = ab.shape[1:]
    hid, lanes = pk.shape[1:]
    dma = pltpu.SemaphoreType.DMA
    return pl.pallas_call(
        gather_kernel,
        out_shape=(
            jax.ShapeDtypeStruct((4, 4, hid, lanes), BF),
            jax.ShapeDtypeStruct((2, 4, n_tok, width), BF),
        ),
        in_specs=[pl.BlockSpec(memory_space=pltpu.VMEM)] * 2,
        out_specs=(pl.BlockSpec(memory_space=pl.ANY),) * 2,
        scratch_shapes=[
            dma((3,)),
            dma((3,)),
            dma((3,)),
            dma((2, 3, 4)),
            dma((2, 3, 4)),
            dma((2, 2)),
            dma((2, 2)),
            dma((2, 2)),
            dma((2, 2)),
            dma((2, 3, 2)),
            dma((2, 3, 2)),
            dma((2, 3, 4)),
            dma((2, 3, 4)),
        ],
        compiler_params=pltpu.CompilerParams(
            collective_id=1, has_side_effects=True, vmem_limit_bytes=60 * 2**20
        ),
        name="gather_all",
    )(pk, ab)


def reduce_kernel(
    pp, qq, jo, do, mods, flag,
    ob, gn, gr,
    R, X1, F1, X2, F2, RB, Z, O, FIN, ZR, ZL, YN, ZN, GN,
    lsem, cs, cr, e1s, e1r, e2s, e2r, hs, hr, hs2, hr2, zs, zr, ws, wr, ags, agr, ags2, agr2, abs_, abr,
    gys, gyr, gzs, gzr, gxs, gxr, gbs, gbr,
):
    zl, y, x, zh, c = (lax.axis_index(n) for n in AXES)
    meet(
        [{"y": lax.rem(y + d, 4)} for d in (1, 2, 3)]
        + [{"x": lax.rem(x + d, 4)} for d in (1, 2, 3)]
        + [along_z(zl, zh, d) for d in (1, -1, 2, -2, 3, -3)]
        + [{"c": 1 - c}]
    )
    xp, xo, xm = lax.rem(x + 1, 4), lax.rem(x + 2, 4), lax.rem(x + 3, 4)
    first = c == 0
    p1 = jnp.where(first, y, x)
    p2 = jnp.where(first, x, y)
    n_r, width = pp.shape[4:]
    step_r = 16
    blocks = n_r // step_r
    tail = []

    def start(cp, ok=None):
        cp.start()
        tail.append((ok, cp))

    def nb(stage, sign):
        s = sign % 4
        along_y = first if stage == 1 else c == 1
        return {
            "y": jnp.where(along_y, lax.rem(y + s, 4), y),
            "x": jnp.where(along_y, x, lax.rem(x + s, 4)),
        }

    def zpiece(way, k, p, from_input):
        buf = ZR if way == 0 else ZL
        src = qq.at[k, p] if from_input else buf.at[k, p]
        to = zl + 1 if way == 0 else zl - 1
        return remote(src, buf.at[k, p], zs.at[way, k, p], zr.at[way, k, p], zl=to)

    hid = qq.shape[2]

    def q_add(buf, k, p):
        def body(i, carry):
            r = pl.ds(pl.multiple_of(i * 48, 16), 48)
            buf[k, p, r, :] = (buf[k, p, r, :].astype(F32) + qq[k, p, r, :].astype(F32)).astype(BF)
            return carry

        lax.fori_loop(0, hid // 48, body, 0)

    zorder = [(s, p) for s in range(3) for p in range(4)]
    for s, p in zorder:

        @pl.when(zl == 0)
        def _():
            zpiece(0, 3 - s, p, True).start()

        @pl.when(zl == 3)
        def _():
            zpiece(1, s, p, True).start()

    def ztick(s, p):
        for way in (0, 1):
            k = 3 - s if way == 0 else s
            mid = (zl > 0) & (zl < k) if way == 0 else (zl < 3) & (zl > k)

            @pl.when(mid)
            def _():
                zpiece(way, k, p, False).wait_recv()
                q_add(ZR if way == 0 else ZL, k, p)
                zpiece(way, k, p, False).start()

    o_first = c == 1
    op1 = jnp.where(o_first, y, x)
    for d in (2, 1, 3, 0):
        for a in range(2):
            k = lax.rem(op1 + d, 4)
            for j in range(4):
                iy, ix = jnp.where(o_first, k, j), jnp.where(o_first, j, k)
                remote(
                    pp.at[a, iy, 1 - c, ix], R.at[a, k, j], cs.at[a, d], cr.at[a, d], c=1 - c
                ).start()

    def own_sum(a, d):
        k = lax.rem(p1 + d, 4)
        remote(R.at[a, k], R.at[a, k], cs.at[a, d], cr.at[a, d], c=c).wait_recv()

        def body(n, carry):
            j, r = n // blocks, lax.rem(n, blocks)
            iy, ix = jnp.where(first, k, j), jnp.where(first, j, k)
            rr = pl.ds(pl.multiple_of(r * step_r, step_r), step_r)
            R[a, k, j, rr, :] = (
                R[a, k, j, rr, :].astype(F32) + pp[a, iy, c, ix, rr, :].astype(F32)
            ).astype(BF)
            return carry

        lax.fori_loop(0, 4 * blocks, body, 0)

    def view(stage, a, d):
        if stage == 1:
            return R.at[a, lax.rem(p1 + d, 4)]
        return R.at[a, p1, lax.rem(p2 + d, 4)]

    def bufs(stage):
        return (X1, F1, e1s, e1r) if stage == 1 else (X2, F2, e2s, e2r)

    def add_to(dst, *srcs):
        if len(dst.shape) == 3:

            def body(n, carry):
                j, r = n // blocks, lax.rem(n, blocks)
                rr = pl.ds(pl.multiple_of(r * step_r, step_r), step_r)
                total = dst[j, rr, :].astype(F32)
                for s in srcs:
                    total = total + s[j, rr, :].astype(F32)
                dst[j, rr, :] = total.astype(BF)
                return carry

            lax.fori_loop(0, dst.shape[0] * blocks, body, 0)
        else:

            def body(r, carry):
                rr = pl.ds(pl.multiple_of(r * step_r, step_r), step_r)
                total = dst[rr, :].astype(F32)
                for s in srcs:
                    total = total + s[rr, :].astype(F32)
                dst[rr, :] = total.astype(BF)
                return carry

            lax.fori_loop(0, blocks, body, 0)

    def ring_first(stage, a):
        X, F, es, er = bufs(stage)
        sg = 1 if a == 0 else -1
        start(remote(view(stage, a, 2), X.at[a], es.at[a, 0], er.at[a, 0], **nb(stage, sg)))

    def ring_own(stage, a):
        X, F, es, er = bufs(stage)
        sg = 1 if a == 0 else -1
        start(remote(view(stage, a, -sg % 4), F.at[1, a], es.at[a, 1], er.at[a, 1], **nb(stage, -sg)))

    def ring_pass(stage, a):
        X, F, es, er = bufs(stage)
        sg = 1 if a == 0 else -1
        cp = remote(X.at[a], X.at[a], es.at[a, 0], er.at[a, 0], c=c)
        cp.wait_recv()
        mine = view(stage, a, sg % 4)
        add_to(mine, X.at[a])
        start(remote(mine, F.at[0, a], es.at[a, 2], er.at[a, 2], **nb(stage, sg)))

    def ring_last(stage, a):
        X, F, es, er = bufs(stage)
        remote(F.at[1, a], F.at[1, a], es.at[a, 1], er.at[a, 1], c=c).wait_recv()
        remote(F.at[0, a], F.at[0, a], es.at[a, 2], er.at[a, 2], c=c).wait_recv()
        add_to(view(stage, a, 0), F.at[0, a], F.at[1, a])

    own_sum(1, 2)
    ring_first(1, 1)
    own_sum(0, 2)
    ring_first(1, 0)
    ztick(0, 0)
    own_sum(0, 3)
    ring_own(1, 0)
    own_sum(1, 1)
    ring_own(1, 1)
    ztick(0, 1)
    own_sum(1, 3)
    own_sum(0, 1)
    own_sum(1, 0)
    own_sum(0, 0)
    ztick(0, 2)
    ring_pass(1, 1)
    ring_pass(1, 0)
    ztick(0, 3)
    for p in range(4):
        ztick(1, p)
    for a in (1, 0):
        ring_last(1, a)
        ring_first(2, a)
        ring_own(2, a)
    for a in (1, 0):
        ring_pass(2, a)

    hr_n = n_r // 2

    def half_rows(way):
        return pl.ds(way * hr_n, hr_n)

    def zh_send(a, way):
        mine = R.at[a, p1, p2, half_rows(way)]
        return remote(mine, RB.at[a, way], hs.at[a, way], hr.at[a, way], **along_z(zl, zh, (1, -1)[way]))

    def zh_pass(a, way):
        return remote(
            RB.at[a, way], Z.at[a, half_rows(way)], hs2.at[a, way], hr2.at[a, way], **along_z(zl, zh, (3, -3)[way])
        )

    for a in (1, 0):
        ring_last(2, a)
        for way in (0, 1):
            start(zh_send(a, way))

    def wcopy(d):
        to = lax.rem(y + d, 4)
        return remote(FIN.at[to], gr.at[y], ws.at[d], wr.at[d], y=to)

    def grad_final(d):
        p = lax.rem(y + d, 4)

        @pl.when(zl > 0)
        def _():
            remote(ZR.at[zl, p], ZR.at[zl, p], zs.at[0, zl, p], zr.at[0, zl, p], c=c).wait_recv()

        @pl.when(zl < 3)
        def _():
            remote(ZL.at[zl, p], ZL.at[zl, p], zs.at[1, zl, p], zr.at[1, zl, p], c=c).wait_recv()

        def body(i, carry):
            r = pl.ds(pl.multiple_of(i * 48, 16), 48)
            zero = jnp.zeros((48, qq.shape[3]), F32)
            total = qq[zl, p, r, :].astype(F32)
            total = total + jnp.where(zl > 0, ZR[zl, p, r, :].astype(F32), zero)
            total = total + jnp.where(zl < 3, ZL[zl, p, r, :].astype(F32), zero)
            FIN[p, r, :] = total.astype(BF)
            return carry

        lax.fori_loop(0, hid // 48, body, 0)
        if d:
            start(wcopy(d))

    for d in (2, 1, 3, 0):
        grad_final(d)
    loc_gr = pltpu.make_async_copy(FIN.at[y], gr.at[y], lsem.at[0])
    loc_gr.start()

    for a in (1, 0):
        for way in (0, 1):
            remote(RB.at[a, way], RB.at[a, way], hs.at[a, way], hr.at[a, way], c=c).wait_recv()
            start(zh_pass(a, way))

    blk = c * 4 + x
    row0 = blk * n_r
    n_text = YN.shape[1]

    def rows_done(a):
        for way in (0, 1):
            part = Z.at[a, half_rows(way)]
            remote(part, part, hs2.at[a, way], hr2.at[a, way], c=c).wait_recv()

        def body(r, carry):
            rr = pl.ds(pl.multiple_of(r * 16, 16), 16)
            at = pl.ds(pl.multiple_of(row0 + r * 16, 16), 16)
            total = R[a, p1, p2, rr, :].astype(F32) + Z[a, rr, :].astype(F32)
            tok = jo[at, :].astype(F32)
            if a == 0:
                O[0, rr, :] = (tok + mods[2:3, :] * total).astype(BF)
            else:
                cen = tok - jnp.mean(tok, axis=-1, keepdims=True)
                inv = lax.rsqrt(jnp.mean(cen * cen, axis=-1, keepdims=True) + EPS)
                normed = cen * inv
                dn = total * (1.0 + mods[1:2, :])
                full = do[at, :].astype(F32) + inv * (
                    dn
                    - jnp.mean(dn, axis=-1, keepdims=True)
                    - normed * jnp.mean(dn * normed, axis=-1, keepdims=True)
                )
                O[1, rr, :] = full.astype(BF)

                @pl.when(r == 0)
                def _():
                    YN[y] = jnp.where(flag[0:1, :] > 0.5, full[:n_text], 0.0).astype(BF)

            return carry

        lax.fori_loop(0, n_r // 16, body, 0)

    locs = [loc_gr]

    def gather_start(a):
        for way, to in ((0, xp), (1, xm)):
            start(remote(O.at[a], ob.at[a, blk], ags.at[a, way], agr.at[a, way], x=to))
        start(remote(O.at[a], ob.at[a, blk], abs_.at[a, 0], abr.at[a, 0], c=1 - c))
        cp = pltpu.make_async_copy(O.at[a], ob.at[a, blk], lsem.at[1 + a])
        cp.start()
        locs.append(cp)

    def gather_near(a):
        for way, frm in ((0, xm), (1, xp)):
            part = ob.at[a, c * 4 + frm]
            remote(part, part, ags.at[a, way], agr.at[a, way], x=x).wait_recv()
            if way == a:
                start(remote(part, part, ags2.at[a], agr2.at[a], x=(xp, xm)[way]))
            start(remote(part, part, abs_.at[a, 1 + way], abr.at[a, 1 + way], c=1 - c))

    def gather_far(a):
        part = ob.at[a, c * 4 + xo]
        remote(part, part, ags2.at[a], agr2.at[a], x=x).wait_recv()
        start(remote(part, part, abs_.at[a, 3], abr.at[a, 3], c=1 - c))

    def gy(d):
        return remote(YN.at[y], YN.at[y], gys.at[d], gyr.at[d], y=lax.rem(y + d, 4))

    def gz(d):
        return remote(ZN.at[zl], ZN.at[zl], gzs.at[d], gzr.at[d], zl=lax.rem(zl + d, 4))

    def gx(d):
        return remote(GN, gn.at[blk], gxs.at[d], gxr.at[d], x=lax.rem(x + d, 4))

    def sum_slots(src, dst):
        total = src[0].astype(F32)
        for i in range(1, 4):
            total = total + src[i].astype(F32)
        dst[...] = total.astype(BF)

    def got(buf, me, sems, semr):
        for d in (1, 3, 2):
            slot = buf.at[lax.rem(me + 4 - d, 4)]
            remote(slot, slot, sems.at[d], semr.at[d], c=c).wait_recv()

    rows_done(1)
    for d in (2, 1, 3):
        start(gy(d))
    gather_start(1)
    got(YN, y, gys, gyr)
    sum_slots(YN, ZN.at[zl])
    for d in (1, 2, 3):
        start(gz(d))
    rows_done(0)
    gather_start(0)
    gather_near(1)
    got(ZN, zl, gzs, gzr)
    sum_slots(ZN, GN)
    for d in (2, 1, 3):
        start(gx(d))
    start(remote(GN, gn.at[blk], gbs.at[0], gbr.at[0], c=1 - c))
    loc_gn = pltpu.make_async_copy(GN, gn.at[blk], lsem.at[3])
    loc_gn.start()
    locs.append(loc_gn)
    gather_far(1)
    gather_near(0)
    for d in (1, 3, 2):
        part = gn.at[c * 4 + lax.rem(x + 4 - d, 4)]
        remote(part, part, gxs.at[d], gxr.at[d], x=x).wait_recv()
        start(remote(part, part, gbs.at[d], gbr.at[d], c=1 - c))
    gather_far(0)
    for d in range(4):
        part = gn.at[(1 - c) * 4 + lax.rem(x + 4 - d, 4)]
        remote(part, part, gbs.at[d], gbr.at[d], c=c).wait_recv()

    for a in range(2):
        for i, frm in enumerate((x, xm, xp, xo)):
            part = ob.at[a, (1 - c) * 4 + frm]
            remote(part, part, abs_.at[a, i], abr.at[a, i], c=c).wait_recv()
    for d in (1, 2, 3):
        frm = gr.at[lax.rem(y + 4 - d, 4)]
        remote(frm, frm, ws.at[d], wr.at[d], y=y).wait_recv()
    for cp in locs:
        cp.wait()
    for _, cp in tail:
        cp.wait_send()
    for d in (2, 1, 3, 0):
        for a in range(2):
            remote(R.at[a, 0], R.at[a, 0], cs.at[a, d], cr.at[a, d], c=1 - c).wait_send()
    for s, p in zorder:
        for way in (0, 1):
            k = 3 - s if way == 0 else s
            did = zl < k if way == 0 else zl > k

            @pl.when(did)
            def _():
                zpiece(way, k, p, False).wait_send()


def reduce_all(pp, qq, jo, do, mods, flag):
    n_r, width = pp.shape[4:]
    hid, lanes = qq.shape[2:]
    dma = pltpu.SemaphoreType.DMA
    vm = pl.BlockSpec(memory_space=pltpu.VMEM)
    hbm = pl.BlockSpec(memory_space=pl.ANY)
    blk = (n_r, width)
    return pl.pallas_call(
        reduce_kernel,
        out_shape=(
            jax.ShapeDtypeStruct((2, 8, *blk), BF),
            jax.ShapeDtypeStruct((8, n_r // 4, width), BF),
            jax.ShapeDtypeStruct((4, hid, lanes), BF),
        ),
        in_specs=[vm] * 6,
        out_specs=(hbm,) * 3,
        scratch_shapes=[
            pltpu.VMEM((2, 4, 4, *blk), BF),
            pltpu.VMEM((2, 4, *blk), BF),
            pltpu.VMEM((2, 2, 4, *blk), BF),
            pltpu.VMEM((2, *blk), BF),
            pltpu.VMEM((2, 2, *blk), BF),
            pltpu.VMEM((2, 2, n_r // 2, width), BF),
            pltpu.VMEM((2, *blk), BF),
            pltpu.VMEM((2, *blk), BF),
            pltpu.VMEM((4, hid, lanes), BF),
            pltpu.VMEM((4, 4, hid, lanes), BF),
            pltpu.VMEM((4, 4, hid, lanes), BF),
            pltpu.VMEM((4, n_r // 4, width), BF),
            pltpu.VMEM((4, n_r // 4, width), BF),
            pltpu.VMEM((n_r // 4, width), BF),
            dma((4,)),
            dma((2, 4)),
            dma((2, 4)),
            dma((2, 3)),
            dma((2, 3)),
            dma((2, 3)),
            dma((2, 3)),
            dma((2, 2)),
            dma((2, 2)),
            dma((2, 2)),
            dma((2, 2)),
            dma((2, 4, 4)),
            dma((2, 4, 4)),
            dma((4,)),
            dma((4,)),
            dma((2, 2)),
            dma((2, 2)),
            dma((2,)),
            dma((2,)),
            dma((2, 4)),
            dma((2, 4)),
            dma((4,)),
            dma((4,)),
            dma((4,)),
            dma((4,)),
            dma((4,)),
            dma((4,)),
            dma((4,)),
            dma((4,)),
        ],
        compiler_params=pltpu.CompilerParams(
            collective_id=2, has_side_effects=True, vmem_limit_bytes=60 * 2**20
        ),
        name="reduce_all",
    )(pp, qq, jo, do, mods, flag)


def dot(left, right, dims):
    return lax.dot_general(left, right, (dims, ((), ())), preferred_element_type=F32)


def mlp_kernel(g, t, pp, qq, up, dn, gu, gd):
    m = pl.program_id(0)
    width = up.shape[1]
    hid, lanes = g.shape[1:]
    part = lanes // 2
    pairs = g.shape[0] // 2

    @pl.when(m == 0)
    def _():
        for j in range(pairs):
            at = slice(j * lanes, (j + 1) * lanes)
            up[:, at] = jnp.concatenate([g[2 * j, :, :part], g[2 * j + 1, :, :part]], axis=1)
            dn[:, at] = jnp.concatenate([g[2 * j, :, part:], g[2 * j + 1, :, part:]], axis=1)
        gu[...] = jnp.zeros_like(gu)
        gd[...] = jnp.zeros_like(gd)

    pre = dot(t[0, 0], up[...], ((1,), (1,)))
    act, gelu_back = jax.vjp(gelu_tanh, pre)
    hidden = act.astype(BF)
    d_pre = gelu_back(dot(t[1, 0], dn[...], ((1,), (1,))))[0].astype(BF)
    cols = width // 4
    for n in range(4):
        at = slice(n * cols, (n + 1) * cols)
        pp[0, 0, :, :, :, at] = dot(hidden, dn[:, at], ((1,), (0,))).astype(BF).reshape(*pp.shape[2:5], cols)
        pp[1, 0, :, :, :, at] = dot(d_pre, up[:, at], ((1,), (0,))).astype(BF).reshape(*pp.shape[2:5], cols)
        gu[:, at] += dot(d_pre, t[0, 0, :, at], ((0,), (0,)))
        gd[:, at] += dot(hidden, t[1, 0, :, at], ((0,), (0,)))

    @pl.when(m == pl.num_programs(0) - 1)
    def _():
        for j in range(pairs):
            u = gu[:, j * lanes : (j + 1) * lanes].astype(BF)
            d = gd[:, j * lanes : (j + 1) * lanes].astype(BF)
            qq[2 * j] = jnp.concatenate([u[:, :part], d[:, :part]], axis=1)
            qq[2 * j + 1] = jnp.concatenate([u[:, part:], d[:, part:]], axis=1)


def mlp(g, t):
    hid, lanes = g.shape[2:]
    n_tok, width = t.shape[2:]
    flops = 12 * 4 * n_tok * width * hid
    return pl.pallas_call(
        mlp_kernel,
        grid=(4,),
        out_shape=(
            jax.ShapeDtypeStruct((2, 4, 2, 4, n_tok // 8, width), BF),
            jax.ShapeDtypeStruct((16, hid, lanes), BF),
        ),
        in_specs=[
            pl.BlockSpec((16, hid, lanes), lambda m: (0, 0, 0)),
            pl.BlockSpec((2, 1, n_tok, width), lambda m: (0, m, 0, 0)),
        ],
        out_specs=(
            pl.BlockSpec((2, 1, 2, 4, n_tok // 8, width), lambda m: (0, m, 0, 0, 0, 0)),
            pl.BlockSpec((16, hid, lanes), lambda m: (0, 0, 0)),
        ),
        scratch_shapes=[
            pltpu.VMEM((hid, width), BF),
            pltpu.VMEM((hid, width), BF),
            pltpu.VMEM((hid, width), F32),
            pltpu.VMEM((hid, width), F32),
        ],
        compiler_params=pltpu.CompilerParams(vmem_limit_bytes=60 * 2**20),
        cost_estimate=pl.CostEstimate(flops=flops, bytes_accessed=30 * 2**20, transcendentals=0),
        name="mlp",
    )(g.reshape(16, hid, lanes), t)


def shards(
    image_tokens, text_tokens, null_prompt, drop_flags, time_index, modulation, w_up, w_down, d_output
):
    dropped = drop_flags == 1
    text_in = jnp.where(dropped[:, None, None], null_prompt[None], text_tokens)[0]
    n_text = text_in.shape[0]

    def blocked(text, image):
        wide = text.shape[-1]
        both = [text.reshape(8, -1, wide), image.reshape(8, -1, wide)]
        return jnp.concatenate(both, axis=1).reshape(-1, wide)

    def in_order(rows):
        wide = rows.shape[-1]
        parts = [rows[:, : n_text // 8], rows[:, n_text // 8 :]]
        return jnp.concatenate([p.reshape(-1, wide) for p in parts], axis=0)[None]

    joined = blocked(text_in, image_tokens[0])
    d_out = blocked(d_output[0, :n_text], d_output[0, n_text:])
    mods = lax.dynamic_index_in_dim(modulation, time_index[0], 0, keepdims=False)
    shift, scale, gate = mods[0:1], mods[1:2], mods[2:3]
    length, width = joined.shape
    joined32 = joined.astype(F32)
    centred = joined32 - jnp.mean(joined32, axis=-1, keepdims=True)
    inv_std = lax.rsqrt(jnp.mean(centred * centred, axis=-1, keepdims=True) + EPS)
    mod_in = (centred * inv_std * (1.0 + scale) + shift).astype(BF)
    d_branch = (d_out.astype(F32) * gate).astype(BF)

    d_part, hid_all = w_up.shape
    hid = hid_all // 4
    pk = jnp.concatenate([w_up.T, w_down], axis=1).reshape(4, hid, 2 * d_part)
    g, t = gather(pk, jnp.stack([mod_in, d_branch]))
    pp, qq = mlp(g, t)
    qq = qq.reshape(4, 4, hid, 2 * d_part)
    flag = jnp.broadcast_to(dropped.astype(F32)[:, None], (1, width))
    ob, gn, gr = reduce_all(pp, qq, joined, d_out, mods, flag)
    grads = gr.reshape(hid_all, 2 * d_part).astype(F32)
    return (
        in_order(ob[0]),
        in_order(ob[1]),
        grads[:, :d_part].T,
        grads[:, d_part:],
        gn.reshape(null_prompt.shape).astype(F32),
    )


def solution(mesh):
    torus = Mesh(mesh.devices.reshape(4, 4, 4, 2, 2), AXES)
    in_specs = (
        P(DP, None, None),
        P(DP, None, None),
        P(),
        P(DP),
        P(DP),
        P(),
        P(DP, MP),
        P(MP, DP),
        P(DP, None, None),
    )
    out_specs = (P(DP, None, None), P(DP, None, None), P(DP, MP), P(MP, DP), P())
    return jax.shard_map(shards, mesh=torus, in_specs=in_specs, out_specs=out_specs, check_vma=False)
```

profile of v0, /device:TPU:1, one launch (start us, length us, event | category | flops | bytes accessed | tf_op | source)
XLA Modules:
  0.0 204.1 jit_solution(13222071005687100099)
XLA Ops:
  0.6 0.0 copy-start.2
  1.4 1.2 fusion.5
  2.6 0.0 copy-done.2
  2.6 0.3 convert_reduce_fusion
  2.9 0.6 multiply_reduce_fusion
  3.4 0.1 rsqrt.12
  4.2 1.0 dynamic-slice_add_fusion
  5.2 2.6 %pad_maximum_fusion.1 = (bf16[8,32,3072]{2,1,0:T(8,128)(2,1)}, f32[8,32,3072]{2,1,0:T(8,128)}) fusion(bf16[8,24,3072]{2,1,0:T(8,128)(2,1)S(1)} %bitcast.67, bf16[8,8,3072]{2,1,0:T(8,128)(2,1)S(1)} %fusion.5), kind=kLoop, calls=%fused_computation.9 | loop fusion | flops 3932160 | bytes 6291456 | tf_op jit(solution)/shard_map/concatenate | solution.py:765
  7.8 0.0 copy-start.3
  7.8 0.1 div.9
  7.9 0.0 slice-start
  7.9 1.3 copy-done.3
  9.2 0.3 slice-done
  9.6 0.0 copy-start.1
  9.6 0.1 pad_maximum_fusion.2
  9.7 0.0 copy-start
  9.7 2.3 %copy-done.1 = f32[8,32,3072]{2,1,0:T(8,128)S(1)} copy-done((f32[8,32,3072]{2,1,0:T(8,128)S(1)}, f32[8,32,3072]{2,1,0:T(8,128)}, u32[]{:S(2)}) %copy-start.1) | copy-done | bytes 3145752
  12.0 1.1 fusion
  13.1 0.0 copy-done
  13.1 0.0 copy-start.6
  13.1 0.0 copy-start.7
  13.2 1.9 pad_maximum_fusion.ab
  15.1 0.0 copy-done.6
  15.1 0.0 copy-done.7
  15.1 1.1 copy.17
  16.2 58.9 %gather_all.1 = (bf16[4,4,192,384]{3,2,1,0:T(8,128)(2,1)}, bf16[2,4,256,3072]{3,2,1,0:T(8,128)(2,1)}) custom-call(bf16[4,192,384]{2,1,0:T(8,128)(2,1)} %bitcast.72, bf16[2,256,3072]{2,1,0:T(8,128)(2,1)} %pad_maximum_fusion.ab), custom_call_target="tpu_custom_call" | custom-call | tf_op jit(solution)/shard_map/gather_all/pallas_call | solution.py:211
  75.0 17.5 %mlp.1 = (bf16[2,4,2,4,32,3072]{5,4,3,2,1,0:T(8,128)(2,1)}, bf16[16,192,384]{2,1,0:T(8,128)(2,1)}) custom-call(bf16[16,192,384]{2,1,0:T(8,128)(2,1)} %bitcast.80, bf16[2,4,256,3072]{3,2,1,0:T(8,128)(2,1)} %get-tuple-element.13.t), custom_call_target="tpu_custom_call" | custom-call | flops 7247757312 | bytes 31457280 | tf_op jit(solution)/shard_map/mlp/pallas_call | solution.py:728
  92.5 1.0 constant_dynamic-slice_fusion.2
  93.5 0.6 copy.24
  94.2 0.6 broadcast_in_dim.34.flag
  94.8 100.9 %reduce_all.1 = (bf16[2,8,32,3072]{3,2,1,0:T(8,128)(2,1)}, bf16[8,8,3072]{2,1,0:T(8,128)(2,1)}, bf16[4,192,384]{2,1,0:T(8,128)(2,1)}) custom-call(bf16[2,4,2,4,32,3072]{5,4,3,2,1,0:T(8,128)(2,1)} %get-tuple-element.14.pp, bf16[4,4,192,384]{3,2,1,0:T(8,128)(2,1)} %bitcast.73, bf16[256,3072]{1,0:T(8,128)(2,1)} %bitcast.68, bf16[256,3072]{1,0:T(8,128)(2,1)} %bitcast.63, ...), custom_call_target="tpu_custom_call" | custom-call | tf_op jit(solution)/shard_map/reduce_all/pallas_call | solution.py:622
  195.7 2.2 %slice_bitcast_fusion = (bf16[8,32,3072]{2,1,0:T(8,128)(2,1)S(1)}, bf16[8,32,3072]{2,1,0:T(8,128)(2,1)S(1)}) fusion(bf16[2,8,32,3072]{3,2,1,0:T(8,128)(2,1)} %get-tuple-element.16), kind=kLoop, calls=%fused_computation.14 | loop fusion | bytes 6291456 | tf_op jit(solution)/shard_map/squeeze | solution.py:794
  197.9 0.1 slice.58
  198.0 1.2 maximum_bitcast_fusion.1
  199.2 0.1 slice.56
  199.4 0.0 copy-start.4
  199.4 1.2 maximum_bitcast_fusion
  200.6 0.0 copy-done.4
  200.6 0.1 bitcast_convert_fusion
  200.8 0.3 fusion.7
  201.1 0.0 copy-start.5
  201.1 1.1 copy.21
  202.1 1.1 copy.22
  203.2 0.0 copy-done.5
  203.2 0.9 bitcast_convert_fusion.1
  (6 shorter events, 0.1 us)
Async XLA Ops:
  0.6 1.9 copy-start.2
  7.8 1.4 copy-start.3
  7.9 1.7 slice-start
  9.6 2.5 %copy-start.1 = (f32[8,32,3072]{2,1,0:T(8,128)S(1)}, f32[8,32,3072]{2,1,0:T(8,128)}, u32[]{:S(2)}) copy-start(f32[8,32,3072]{2,1,0:T(8,128)} %get-tuple-element.22) | copy-start | bytes 9437188
  9.7 3.5 %copy-start = (bf16[8,32,3072]{2,1,0:T(8,128)(2,1)}, bf16[8,32,3072]{2,1,0:T(8,128)(2,1)S(1)}, u32[]{:S(2)}) copy-start(bf16[8,32,3072]{2,1,0:T(8,128)(2,1)S(1)} %pad_maximum_fusion.2) | copy-start | bytes 4718596
  13.1 1.9 copy-start.6
  13.1 1.9 copy-start.7
  199.4 1.3 copy-start.4
  201.1 2.1 %copy-start.5 = (bf16[8,8,3072]{2,1,0:T(8,128)(2,1)S(1)}, bf16[8,8,3072]{2,1,0:T(8,128)(2,1)}, u32[]{:S(2)}) copy-start(bf16[8,8,3072]{2,1,0:T(8,128)(2,1)} %get-tuple-element.18) | copy-start | bytes 1179652
where the time goes:
time: 207 us; the launch traced here: 204 us
  Pallas kernels  177 us (86%)
  local copies, waits for them, and re-layouts  12.3 us (6%)
  other arithmetic  12.3 us (6%)
  between operations  2.2 us (1%)
    pallas_call x1, Pallas kernels, reduce_all(): pl.pallas_call(reduce_kernel, out_shape=(jax.ShapeDtypeStruct((2, 8, *blk...  101 us
    pallas_call x1, Pallas kernels, gather(): pl.pallas_call(gather_kernel, out_shape=(jax.ShapeDtypeStruct((4, 4, hid,...  58.9 us
    pallas_call x1, Pallas kernels, mlp(): pl.pallas_call(mlp_kernel, grid=(4,), out_shape=(jax.ShapeDtypeStruct((2,...  17.5 us
    unnamed x19, local copies, waits for them, and re-layouts  6.46 us

commit v1 on v0

v1 whole, which is shorter than its diff:
```python
import jax
import jax.numpy as jnp
from jax import lax
from jax.experimental import pallas as pl
from jax.experimental.pallas import tpu as pltpu
from jax.sharding import Mesh
from jax.sharding import PartitionSpec as P

AXES = ("zl", "y", "x", "zh", "c")
MP = ("x", "zh", "c")
DP = ("zl", "y")
EPS = 1e-06
MESH = pl.DeviceIdType.MESH
BF = jnp.bfloat16
F32 = jnp.float32


def gelu_tanh(values):
    return jax.nn.gelu(values, approximate=True)


def remote(src, dst, ss, rs, **dev):
    return pltpu.make_async_remote_copy(
        src_ref=src, dst_ref=dst, send_sem=ss, recv_sem=rs, device_id=dev, device_id_type=MESH
    )


def meet(devices):
    barrier = pltpu.get_barrier_semaphore()
    for dev in devices:
        pl.semaphore_signal(barrier, inc=1, device_id=dev, device_id_type=MESH)
    pl.semaphore_wait(barrier, len(devices))


def along_z(zl, zh, dist):
    to = lax.rem(zh * 4 + zl + dist % 8, 8)
    return {"zl": lax.rem(to, 4), "zh": to // 4}


def dot(left, right, dims):
    return lax.dot_general(left, right, (dims, ((), ())), preferred_element_type=F32)


def step_kernel(
    pk, jo, do, mods,
    ob, gn, gr,
    t, g, up, dn, PA, HD, pp, qq,
    R, X1, F1, X2, F2, RB, Z, O, FIN, ZR, ZL, YN, ZN, GN, JD,
    lsem, gws0, gwr0, gzs0, gzr0, ys, yr, ps, pr, xs, xr, bs, br,
    cs, cr, e1s, e1r, e2s, e2r, hs, hr, hs2, hr2, zs, zr, ws, wr, ags, agr, ags2, agr2, abs_, abr,
    gys, gyr, gzs, gzr, gxs, gxr, gbs, gbr,
):
    zl, y, x, zh, c = (lax.axis_index(n) for n in AXES)
    meet(
        [{"y": lax.rem(y + d, 4)} for d in (1, 2, 3)]
        + [{"x": lax.rem(x + d, 4)} for d in (1, 2, 3)]
        + [along_z(zl, zh, d) for d in (1, -1, 2, -2, 3, -3)]
        + [{"c": 1 - c}]
    )
    yp, yo, ym = lax.rem(y + 1, 4), lax.rem(y + 2, 4), lax.rem(y + 3, 4)
    xp, xo, xm = lax.rem(x + 1, 4), lax.rem(x + 2, 4), lax.rem(x + 3, 4)
    qrt = jo.shape[0] // 4
    half = qrt // 2
    par = lax.rem(x, 2)
    peers = (ym, yp, yo)
    sent = []

    def rows(quarter, h, n=1):
        return pl.ds(pl.multiple_of(quarter * qrt + h * half, half), n * half)

    own_q = par * 2 + c
    x_q = (1 - par) * 2 + c
    sib_q = (par * 2 + (1 - c), (1 - par) * 2 + (1 - c))

    def w1(d):
        to = lax.rem(y + d, 4)
        return remote(pk.at[to], g.at[zl, y], gws0.at[d - 1], gwr0.at[d - 1], y=to)

    for d in (1, 3, 2):
        w1(d).start()
        sent.append((None, w1(d)))
    pk_own = pltpu.make_async_copy(pk.at[y], g.at[zl, y], lsem.at[0])
    pk_own.start()
    n_r = O.shape[1]
    blk = c * 4 + x
    loads = [pltpu.make_async_copy(r, JD.at[i], lsem.at[3 + i]) for i, r in enumerate((jo, do))]
    for cp in loads:
        cp.start()

    def norm_of(tok):
        cen = tok - jnp.mean(tok, axis=-1, keepdims=True)
        inv = lax.rsqrt(jnp.mean(cen * cen, axis=-1, keepdims=True) + EPS)
        return cen * inv, inv

    def zcopy(way, s, d):
        yd = lax.rem(y + 4 - d, 4)
        block = zl - s if way == 0 else zl + s
        src = pk.at[y] if (s == 0 and d == 0) else g.at[block, yd]
        to = zl + 1 if way == 0 else zl - 1
        return remote(src, g.at[block, yd], gzs0.at[way, s, d], gzr0.at[way, s, d], zl=to)

    def zsend(way, s, d):
        ok = (zl < 3) & (zl >= s) if way == 0 else (zl > 0) & (zl + s <= 3)

        @pl.when(ok)
        def _():
            zcopy(way, s, d).start()

        sent.append((ok, (way, s, d)))

    def gtick(s, d):
        for way in (0, 1):
            got = zl >= s if way == 0 else zl + s <= 3
            yd = lax.rem(y + 4 - d, 4)

            @pl.when(got)
            def _():
                block = zl - s if way == 0 else zl + s
                remote(
                    g.at[block, yd], g.at[block, yd], gzs0.at[way, s - 1, d], gzr0.at[way, s - 1, d], zl=zl
                ).wait_recv()

            if s <= 2:
                zsend(way, s, d)

    def wstep(d):
        if d:
            w1(d).wait_recv()
        for way in (0, 1):
            zsend(way, 0, d)

    wstep(0)

    def send_own(a):
        for way, to in ((0, yp), (1, ym)):
            src = t.at[a, y, rows(own_q, 0, 2)]
            cp = remote(src, src, ys.at[a, way], yr.at[a, way], y=to)
            cp.start()
            sent.append((None, cp))

    def ready(a, first_block, n_blocks):
        def body(i, carry):
            at = lax.rem(own_q * qrt + (first_block + i) * 16, 4 * qrt)
            rr = pl.ds(pl.multiple_of(at, 16), 16)
            val = JD[a, rr, :].astype(F32)
            if a == 0:
                t[0, y, rr, :] = (norm_of(val)[0] * (1.0 + mods[1:2, :]) + mods[0:1, :]).astype(BF)
            else:
                t[1, y, rr, :] = (val * mods[2:3, :]).astype(BF)
            return carry

        lax.fori_loop(0, n_blocks, body, 0)

    for a in range(2):
        loads[a].wait()
        ready(a, 0, qrt // 16)
        send_own(a)
        if a == 0:
            wstep(1)
            wstep(3)
    for a in range(2):
        ready(a, qrt // 16, 3 * qrt // 16)

    def send_on(a, peer, h):
        src = t.at[a, peers[peer], rows(own_q, h)]
        for cp in (
            remote(src, src, xs.at[a, peer, h], xr.at[a, peer, h], x=(xp, xm)[h]),
            remote(src, src, bs.at[a, peer, h], br.at[a, peer, h], c=1 - c),
        ):
            cp.start()
            sent.append((None, cp))

    def direct(a, way):
        whole = t.at[a, peers[way], rows(own_q, 0, 2)]
        remote(whole, whole, ys.at[a, way], yr.at[a, way], y=y).wait_recv()
        part = t.at[a, peers[way], rows(own_q, way)]
        cp = remote(part, part, ps.at[a, way], pr.at[a, way], y=(yp, ym)[way])
        cp.start()
        sent.append((None, cp))
        for h in (0, 1):
            send_on(a, way, h)

    def relayed(a, h):
        part = t.at[a, yo, rows(own_q, h)]
        remote(part, part, ps.at[a, h], pr.at[a, h], y=y).wait_recv()
        send_on(a, 2, h)

    def from_x(a, peer):
        for h in (0, 1):
            part = t.at[a, peers[peer], rows(x_q, h)]
            remote(part, part, xs.at[a, peer, h], xr.at[a, peer, h], x=x).wait_recv()
            cp = remote(part, part, bs.at[a, peer, 2 + h], br.at[a, peer, 2 + h], c=1 - c)
            cp.start()
            sent.append((None, cp))

    gtick(1, 0)
    wstep(2)
    gtick(1, 1)
    direct(0, 1)
    gtick(1, 3)
    gtick(1, 2)
    direct(0, 0)
    gtick(2, 0)
    direct(1, 1)
    gtick(2, 1)
    relayed(0, 1)
    from_x(0, 1)
    direct(1, 0)
    gtick(2, 3)
    from_x(0, 0)
    gtick(2, 2)
    relayed(1, 1)
    relayed(0, 0)
    gtick(3, 0)
    from_x(1, 1)
    relayed(1, 0)
    gtick(3, 1)
    from_x(1, 0)
    from_x(0, 2)
    gtick(3, 3)
    gtick(3, 2)
    from_x(1, 2)
    for a in range(2):
        for peer in range(3):
            for kind in range(4):
                part = t.at[a, peers[peer], rows(sib_q[kind // 2], kind % 2)]
                remote(part, part, bs.at[a, peer, kind], br.at[a, peer, kind], c=c).wait_recv()
    pk_own.wait()

    first = c == 0
    p1 = jnp.where(first, y, x)
    p2 = jnp.where(first, x, y)
    width = pp.shape[5]
    step_r = 16
    blocks = n_r // step_r

    flying = {}

    def start(cp, key=None):
        cp.start()
        flying[key if key is not None else len(flying) + 1000] = cp

    def drain(*key):
        for w in (0, 1):
            flying.pop((*key, w)).wait_send()

    def nb(stage, sign):
        s = sign % 4
        along_y = first if stage == 1 else c == 1
        return {
            "y": jnp.where(along_y, lax.rem(y + s, 4), y),
            "x": jnp.where(along_y, x, lax.rem(x + s, 4)),
        }

    def zblock(way, k, h, from_input):
        buf = ZR if way == 0 else ZL
        at = pl.ds(2 * h, 2)
        src = qq.at[k, at] if from_input else buf.at[k, at]
        to = zl + 1 if way == 0 else zl - 1
        return remote(src, buf.at[k, at], zs.at[way, k, h], zr.at[way, k, h], zl=to)

    hid = qq.shape[2]
    q_rows = 48

    def q_at(i):
        return i // (hid // q_rows), pl.ds(pl.multiple_of(lax.rem(i, hid // q_rows) * q_rows, 16), q_rows)

    def z_end(n, ways=(0, 1)):
        for way in ways:
            k = 3 - n if way == 0 else n

            @pl.when(zl == 3 * way)
            def _():
                for h in (0, 1):
                    zblock(way, k, h, True).start()

    def z_mid(way, k, who, h):
        buf = ZR if way == 0 else ZL

        @pl.when(zl == who)
        def _():
            zblock(way, k, h, False).wait_recv()

            def body(i, carry):
                p, r = q_at(i)
                p = p + 2 * h
                buf[k, p, r, :] = (buf[k, p, r, :].astype(F32) + qq[k, p, r, :].astype(F32)).astype(BF)
                return carry

            lax.fori_loop(0, 2 * hid // q_rows, body, 0)
            zblock(way, k, h, False).start()

    def own_sum(a, d):
        k = lax.rem(p1 + d, 4)
        remote(R.at[a, k], R.at[a, k], cs.at[a, d], cr.at[a, d], c=c).wait_recv()

        def body(n, carry):
            j, r = n // blocks, lax.rem(n, blocks)
            iy, ix = jnp.where(first, k, j), jnp.where(first, j, k)
            rr = pl.ds(pl.multiple_of(r * step_r, step_r), step_r)
            R[a, k, j, rr, :] = (
                R[a, k, j, rr, :].astype(F32) + pp[a, iy, c, ix, rr, :].astype(F32)
            ).astype(BF)
            return carry

        lax.fori_loop(0, 4 * blocks, body, 0)

    hr_n = n_r // 2

    def half_rows(way):
        return pl.ds(way * hr_n, hr_n)

    def view(stage, a, w, d):
        if stage == 1:
            return R.at[a, lax.rem(p1 + d, 4), :, half_rows(w)]
        return R.at[a, p1, lax.rem(p2 + d, 4), half_rows(w)]

    def bufs(stage):
        return (X1, F1, e1s, e1r) if stage == 1 else (X2, F2, e2s, e2r)

    def add_to(stage, a, w, d, *srcs):
        if stage == 1:
            k = lax.rem(p1 + d, 4)

            def body(j, carry):
                total = R[a, k, j, half_rows(w), :].astype(F32)
                for s in srcs:
                    total = total + s[j].astype(F32)
                R[a, k, j, half_rows(w), :] = total.astype(BF)
                return carry

            lax.fori_loop(0, 4, body, 0)
        else:
            k = lax.rem(p2 + d, 4)
            total = R[a, p1, k, half_rows(w), :].astype(F32)
            for s in srcs:
                total = total + s[...].astype(F32)
            R[a, p1, k, half_rows(w), :] = total.astype(BF)

    def ring_first(stage, a):
        X, F, es, er = bufs(stage)
        for w, sg in ((0, 1), (1, -1)):
            start(
                remote(view(stage, a, w, 2), X.at[a, w], es.at[a, w, 0], er.at[a, w, 0], **nb(stage, sg)),
                (stage, a, 0, w),
            )

    def ring_own(stage, a, w):
        X, F, es, er = bufs(stage)
        sg = (1, -1)[w]
        src = view(stage, a, w, -sg % 4)
        start(
            remote(src, F.at[1, a, w], es.at[a, w, 1], er.at[a, w, 1], **nb(stage, -sg)), (stage, a, 1, w)
        )

    def ring_pass(stage, a):
        X, F, es, er = bufs(stage)
        for w, sg in ((0, 1), (1, -1)):
            remote(X.at[a, w], X.at[a, w], es.at[a, w, 0], er.at[a, w, 0], c=c).wait_recv()
            add_to(stage, a, w, sg % 4, X.at[a, w])
            src = view(stage, a, w, sg % 4)
            start(
                remote(src, F.at[0, a, w], es.at[a, w, 2], er.at[a, w, 2], **nb(stage, sg)),
                (stage, a, 2, w),
            )

    def ring_last(stage, a, w):
        X, F, es, er = bufs(stage)
        remote(F.at[1, a, w], F.at[1, a, w], es.at[a, w, 1], er.at[a, w, 1], c=c).wait_recv()
        remote(F.at[0, a, w], F.at[0, a, w], es.at[a, w, 2], er.at[a, w, 2], c=c).wait_recv()
        add_to(stage, a, w, 0, F.at[0, a, w], F.at[1, a, w])

    def zh_send(a, way):
        mine = R.at[a, p1, p2, half_rows(way)]
        return remote(mine, RB.at[a, way], hs.at[a, way], hr.at[a, way], **along_z(zl, zh, (1, -1)[way]))

    def zh_pass(a):
        for way in (0, 1):
            remote(RB.at[a, way], RB.at[a, way], hs.at[a, way], hr.at[a, way], c=c).wait_recv()
            start(
                remote(
                    RB.at[a, way],
                    Z.at[a, half_rows(way)],
                    hs2.at[a, way],
                    hr2.at[a, way],
                    **along_z(zl, zh, (3, -3)[way]),
                )
            )

    def stage_two(a):
        for w in (0, 1):
            ring_last(1, a, w)
        ring_first(2, a)
        for w in (0, 1):
            ring_own(2, a, w)

    def stage_zh(a):
        for w in (0, 1):
            ring_last(2, a, w)
            start(zh_send(a, w))

    lanes = g.shape[3]
    part = lanes // 2
    n_tok = t.shape[2]
    for j in range(8):
        at = slice(j * lanes, (j + 1) * lanes)
        one, two = g.at[2 * j // 4, 2 * j % 4], g.at[(2 * j + 1) // 4, (2 * j + 1) % 4]
        up[:, at] = jnp.concatenate([one[:, :part], two[:, :part]], axis=1)
        dn[:, at] = jnp.concatenate([one[:, part:], two[:, part:]], axis=1)

    def tok_rows(s):
        return pl.ds(pl.multiple_of(s * n_tok, n_tok), n_tok)

    PA[0] = dot(t[0].reshape(4 * n_tok, width), up[...], ((1,), (1,)))
    PA[1] = dot(t[1].reshape(4 * n_tok, width), dn[...], ((1,), (1,)))

    def hidden_of(i, carry):
        rr = pl.ds(pl.multiple_of(i * 64, 64), 64)
        act, gelu_back = jax.vjp(gelu_tanh, PA[0, rr, :])
        HD[0, rr, :] = act.astype(BF)
        HD[1, rr, :] = gelu_back(PA[1, rr, :])[0].astype(BF)
        return carry

    lax.fori_loop(0, 4 * n_tok // 64, hidden_of, 0)

    def weight_grads(k):
        at = slice(2 * k * lanes, 2 * (k + 1) * lanes)
        u = dot(HD[1], t[0, :, :, at].reshape(4 * n_tok, 2 * lanes), ((0,), (0,))).astype(BF)
        v = dot(HD[0], t[1, :, :, at].reshape(4 * n_tok, 2 * lanes), ((0,), (0,))).astype(BF)
        for p in range(4):
            cut = slice(p * part, (p + 1) * part)
            qq[k, p] = jnp.concatenate([u[:, cut], v[:, cut]], axis=1)

    o_first = c == 1
    op1 = jnp.where(o_first, y, x)

    def token_grads(a):
        weights, kept = (dn, up)[a], HD.at[a]

        def sample(i, carry):
            s = lax.rem(y + jnp.where(i == 0, 2, jnp.where(i == 1, 1, jnp.where(i == 2, 3, 0))), 4)
            cols = width // 4
            for n in range(4):
                at = slice(n * cols, (n + 1) * cols)
                out = dot(kept[tok_rows(s), :], weights[:, at], ((1,), (0,)))
                pp[a, s, :, :, :, at] = out.astype(BF).reshape(2, 4, n_r, cols)
            for xx in range(4):
                k, j = jnp.where(o_first, s, xx), jnp.where(o_first, xx, s)
                d = lax.rem(k + 4 - op1, 4)
                remote(pp.at[a, s, 1 - c, xx], R.at[a, k, j], cs.at[a, d], cr.at[a, d], c=1 - c).start()
            return carry

        lax.fori_loop(0, 4, sample, 0)

    weight_grads(3)
    z_end(0, (0,))
    weight_grads(0)
    z_end(0, (1,))
    weight_grads(2)
    weight_grads(1)
    token_grads(1)
    own_sum(1, 2)
    ring_first(1, 1)
    own_sum(1, 3)
    own_sum(1, 1)
    own_sum(1, 0)
    token_grads(0)
    z_end(1)
    drain(1, 1, 0)
    ring_own(1, 1, 0)
    ring_own(1, 1, 1)
    own_sum(0, 2)
    ring_pass(1, 1)
    own_sum(0, 3)
    own_sum(0, 1)
    own_sum(0, 0)
    drain(1, 1, 1)
    ring_first(1, 0)
    for h in (0, 1):
        z_mid(0, 3, 1, h)
        z_mid(1, 0, 2, h)
    stage_two(1)
    z_end(2)
    drain(1, 0, 0)
    ring_own(1, 0, 0)
    ring_own(1, 0, 1)
    ring_pass(1, 0)
    for h in (0, 1):
        z_mid(0, 2, 1, h)
        z_mid(1, 1, 2, h)
    ring_pass(2, 1)
    stage_zh(1)
    for h in (0, 1):
        z_mid(0, 3, 2, h)
        z_mid(1, 0, 1, h)
    zh_pass(1)
    stage_two(0)
    ring_pass(2, 0)
    stage_zh(0)

    def wcopy(d):
        to = lax.rem(y + d, 4)
        return remote(FIN.at[to], gr.at[y], ws.at[d], wr.at[d], y=to)

    def grad_final(d):
        p = lax.rem(y + d, 4)

        def body(i, carry):
            r = pl.ds(pl.multiple_of(i * 48, 16), 48)
            zero = jnp.zeros((48, qq.shape[3]), F32)
            total = qq[zl, p, r, :].astype(F32)
            total = total + jnp.where(zl > 0, ZR[zl, p, r, :].astype(F32), zero)
            total = total + jnp.where(zl < 3, ZL[zl, p, r, :].astype(F32), zero)
            FIN[p, r, :] = total.astype(BF)
            return carry

        lax.fori_loop(0, hid // 48, body, 0)
        if d:
            start(wcopy(d))

    n_text = YN.shape[1]

    def rows_done(a):
        for way in (0, 1):
            part = Z.at[a, half_rows(way)]
            remote(part, part, hs2.at[a, way], hr2.at[a, way], c=c).wait_recv()

        def body(r, carry):
            rr = pl.ds(pl.multiple_of(r * 16, 16), 16)
            total = R[a, p1, p2, rr, :].astype(F32) + Z[a, rr, :].astype(F32)
            at = pl.ds(pl.multiple_of(blk * n_r + r * 16, 16), 16)
            tok = JD[0, at, :].astype(F32)
            if a == 0:
                O[0, rr, :] = (tok + mods[2:3, :] * total).astype(BF)
            else:
                normed, inv = norm_of(tok)
                dn = total * (1.0 + mods[1:2, :])
                full = JD[1, at, :].astype(F32) + inv * (
                    dn
                    - jnp.mean(dn, axis=-1, keepdims=True)
                    - normed * jnp.mean(dn * normed, axis=-1, keepdims=True)
                )
                O[1, rr, :] = full.astype(BF)

                @pl.when(r == 0)
                def _():
                    YN[y] = jnp.where(mods[3:4, :] > 0.5, full[:n_text], 0.0).astype(BF)

            return carry

        lax.fori_loop(0, n_r // 16, body, 0)

    locs = []

    def gather_start(a):
        for way, to in ((0, xp), (1, xm)):
            start(remote(O.at[a], ob.at[a, blk], ags.at[a, way], agr.at[a, way], x=to))
        start(remote(O.at[a], ob.at[a, blk], abs_.at[a, 0], abr.at[a, 0], c=1 - c))
        cp = pltpu.make_async_copy(O.at[a], ob.at[a, blk], lsem.at[1 + a])
        cp.start()
        locs.append(cp)

    def gather_near(a):
        for way, frm in ((0, xm), (1, xp)):
            part = ob.at[a, c * 4 + frm]
            remote(part, part, ags.at[a, way], agr.at[a, way], x=x).wait_recv()
            piece = ob.at[a, c * 4 + frm, half_rows(way)]
            start(remote(piece, piece, ags2.at[a, way], agr2.at[a, way], x=(xp, xm)[way]))
            start(remote(part, part, abs_.at[a, 1 + way], abr.at[a, 1 + way], c=1 - c))

    def gather_far(a):
        for way in (0, 1):
            piece = ob.at[a, c * 4 + xo, half_rows(way)]
            remote(piece, piece, ags2.at[a, way], agr2.at[a, way], x=x).wait_recv()
            start(remote(piece, piece, abs_.at[a, 3 + way], abr.at[a, 3 + way], c=1 - c))

    def gy(d):
        return remote(YN.at[y], YN.at[y], gys.at[d], gyr.at[d], y=lax.rem(y + d, 4))

    def gz(d):
        return remote(ZN.at[zl], ZN.at[zl], gzs.at[d], gzr.at[d], zl=lax.rem(zl + d, 4))

    def gx(d):
        return remote(GN, gn.at[blk], gxs.at[d], gxr.at[d], x=lax.rem(x + d, 4))

    def sum_slots(src, dst):
        total = src[0].astype(F32)
        for i in range(1, 4):
            total = total + src[i].astype(F32)
        dst[...] = total.astype(BF)

    def got(buf, me, sems, semr):
        for d in (1, 3, 2):
            slot = buf.at[lax.rem(me + 4 - d, 4)]
            remote(slot, slot, sems.at[d], semr.at[d], c=c).wait_recv()

    rows_done(1)
    for d in (2, 1, 3):
        start(gy(d))
    gather_start(1)
    zh_pass(0)
    got(YN, y, gys, gyr)
    sum_slots(YN, ZN.at[zl])
    for d in (1, 2, 3):
        start(gz(d))
    gather_near(1)
    rows_done(0)
    gather_start(0)
    for way in (0, 1):

        @pl.when(zl != 3 * way)
        def _():
            for h in (0, 1):
                zblock(way, zl, h, False).wait_recv()

    for d in (2, 1, 3, 0):
        grad_final(d)
    loc_gr = pltpu.make_async_copy(FIN.at[y], gr.at[y], lsem.at[0])
    loc_gr.start()
    locs.append(loc_gr)
    got(ZN, zl, gzs, gzr)
    sum_slots(ZN, GN)
    for d in (2, 1, 3):
        start(gx(d))
    start(remote(GN, gn.at[blk], gbs.at[0], gbr.at[0], c=1 - c))
    loc_gn = pltpu.make_async_copy(GN, gn.at[blk], lsem.at[3])
    loc_gn.start()
    locs.append(loc_gn)
    gather_far(1)
    gather_near(0)
    for d in (1, 3, 2):
        part = gn.at[c * 4 + lax.rem(x + 4 - d, 4)]
        remote(part, part, gxs.at[d], gxr.at[d], x=x).wait_recv()
        start(remote(part, part, gbs.at[d], gbr.at[d], c=1 - c))
    gather_far(0)
    for d in range(4):
        part = gn.at[(1 - c) * 4 + lax.rem(x + 4 - d, 4)]
        remote(part, part, gbs.at[d], gbr.at[d], c=c).wait_recv()

    for a in range(2):
        for i, frm in enumerate((x, xm, xp, xo, xo)):
            part = ob.at[a, (1 - c) * 4 + frm]
            if i >= 3:
                part = ob.at[a, (1 - c) * 4 + frm, half_rows(i - 3)]
            remote(part, part, abs_.at[a, i], abr.at[a, i], c=c).wait_recv()
    for d in (1, 2, 3):
        frm = gr.at[lax.rem(y + 4 - d, 4)]
        remote(frm, frm, ws.at[d], wr.at[d], y=y).wait_recv()
    for cp in locs:
        cp.wait()
    for cp in flying.values():
        cp.wait_send()
    for d in (2, 1, 3, 0):
        for a in range(2):
            remote(R.at[a, 0], R.at[a, 0], cs.at[a, d], cr.at[a, d], c=1 - c).wait_send()
    for way in (0, 1):
        for k in range(4):

            @pl.when(zl < k if way == 0 else zl > k)
            def _():
                for h in (0, 1):
                    zblock(way, k, h, False).wait_send()

    for ok, cp in sent:
        if ok is None:
            cp.wait_send()
        else:
            way, s, d = cp

            @pl.when(ok)
            def _():
                zcopy(way, s, d).wait_send()


def step(pk, jo, do, mods):
    n_tok, width = jo.shape
    hid, lanes = pk.shape[1:]
    n_r = n_tok // 8
    half, eighth = n_r // 2, n_r // 4
    vm = pl.BlockSpec(memory_space=pltpu.VMEM)
    hbm = pl.BlockSpec(memory_space=pl.ANY)

    def buf(*shape):
        return pltpu.VMEM(shape, BF)

    counts = [(5,), (3,), (3,), (2, 3, 4), (2, 3, 4), (2, 2), (2, 2), (2, 2), (2, 2)]
    counts += [(2, 3, 2), (2, 3, 2), (2, 3, 4), (2, 3, 4)]
    counts += [(2, 4)] * 2 + [(2, 2, 3)] * 4 + [(2, 2)] * 4 + [(2, 4, 2)] * 2 + [(4,)] * 2
    counts += [(2, 2)] * 4 + [(2, 5)] * 2 + [(4,)] * 8
    return pl.pallas_call(
        step_kernel,
        out_shape=(
            jax.ShapeDtypeStruct((2, 8, n_r, width), BF),
            jax.ShapeDtypeStruct((8, eighth, width), BF),
            jax.ShapeDtypeStruct((4, hid, lanes), BF),
        ),
        in_specs=[vm, hbm, hbm, vm],
        out_specs=(hbm,) * 3,
        scratch_shapes=[
            buf(2, 4, n_tok, width),
            buf(4, 4, hid, lanes),
            buf(hid, width),
            buf(hid, width),
            pltpu.VMEM((2, 4 * n_tok, hid), F32),
            buf(2, 4 * n_tok, hid),
            buf(2, 4, 2, 4, n_r, width),
            buf(4, 4, hid, lanes),
            buf(2, 4, 4, n_r, width),
            buf(2, 2, 4, half, width),
            buf(2, 2, 2, 4, half, width),
            buf(2, 2, half, width),
            buf(2, 2, 2, half, width),
            buf(2, 2, half, width),
            buf(2, n_r, width),
            buf(2, n_r, width),
            buf(4, hid, lanes),
            buf(4, 4, hid, lanes),
            buf(4, 4, hid, lanes),
            buf(4, eighth, width),
            buf(4, eighth, width),
            buf(eighth, width),
            buf(2, n_tok, width),
        ]
        + [pltpu.SemaphoreType.DMA(n) for n in counts],
        compiler_params=pltpu.CompilerParams(
            collective_id=1, has_side_effects=True, vmem_limit_bytes=67043328
        ),
        name="step",
    )(pk, jo, do, mods)


def shards(
    image_tokens, text_tokens, null_prompt, drop_flags, time_index, modulation, w_up, w_down, d_output
):
    dropped = drop_flags == 1
    text_in = jnp.where(dropped[:, None, None], null_prompt[None], text_tokens)[0]
    n_text = text_in.shape[0]

    def blocked(text, image):
        wide = text.shape[-1]
        both = [text.reshape(8, -1, wide), image.reshape(8, -1, wide)]
        return jnp.concatenate(both, axis=1).reshape(-1, wide)

    def in_order(rows):
        wide = rows.shape[-1]
        parts = [rows[:, : n_text // 8], rows[:, n_text // 8 :]]
        return jnp.concatenate([p.reshape(-1, wide) for p in parts], axis=0)[None]

    joined = blocked(text_in, image_tokens[0])
    d_out = blocked(d_output[0, :n_text], d_output[0, n_text:])
    width = joined.shape[-1]
    mods = lax.dynamic_index_in_dim(modulation, time_index[0], 0, keepdims=False)
    mods = jnp.concatenate([mods, jnp.broadcast_to(dropped.astype(F32)[:, None], (1, width))], axis=0)

    d_part, hid_all = w_up.shape
    hid = hid_all // 4
    pk = jnp.concatenate([w_up.T, w_down], axis=1).reshape(4, hid, 2 * d_part)
    ob, gn, gr = step(pk, joined, d_out, mods)
    grads = gr.reshape(hid_all, 2 * d_part).astype(F32)
    return (
        in_order(ob[0]),
        in_order(ob[1]),
        grads[:, :d_part].T,
        grads[:, d_part:],
        gn.reshape(null_prompt.shape).astype(F32),
    )


def solution(mesh):
    torus = Mesh(mesh.devices.reshape(4, 4, 4, 2, 2), AXES)
    in_specs = (
        P(DP, None, None),
        P(DP, None, None),
        P(),
        P(DP),
        P(DP),
        P(),
        P(DP, MP),
        P(MP, DP),
        P(DP, None, None),
    )
    out_specs = (P(DP, None, None), P(DP, None, None), P(DP, MP), P(MP, DP), P())
    return jax.shard_map(shards, mesh=torus, in_specs=in_specs, out_specs=out_specs, check_vma=False)
```

time: 207 us -> 168 us (0.81); the launches traced: 204 us -> 167 us
  Pallas kernels: 177 us -> 148 us
  other arithmetic: 12.3 us -> 7.15 us
  local copies, waits for them, and re-layouts: 12.3 us -> 9.97 us
    pallas_call x3 -> x1, Pallas kernels: 177 us -> 148 us  [step(): pl.pallas_call(step_kernel, out_shape=(jax.ShapeDtypeStruct((2, 8, n_r, w...]
    unnamed x19 -> x13, local copies, waits for them, and re-layouts: 6.46 us -> 2.17 us
where the time goes in v1:
time: 168 us; the launch traced here: 167 us
  Pallas kernels  148 us (88%)
  local copies, waits for them, and re-layouts  9.97 us (6%)
  other arithmetic  7.15 us (4%)
  between operations  2.12 us (1%)
    pallas_call x1, Pallas kernels, step(): pl.pallas_call(step_kernel, out_shape=(jax.ShapeDtypeStruct((2, 8, n_r, w...  148 us

profile of v1, /device:TPU:1, one launch (start us, length us, event | category | flops | bytes accessed | tf_op | source)
XLA Modules:
  0.0 167.2 jit_solution(15893647177630875578)
XLA Ops:
  0.6 0.0 copy-start.3
  0.6 0.0 copy-start.4
  2.0 1.0 constant_dynamic-slice_fusion
  3.0 0.6 concatenate.21.mods
  3.7 1.0 fusion
  4.7 0.0 copy-start
  4.7 1.1 slice_bitcast_fusion.4
  5.8 0.0 copy-done.3
  5.8 0.0 copy-done.4
  5.9 1.1 copy.17
  7.0 0.0 copy-done
  7.0 1.3 pad_maximum_fusion
  8.2 0.0 slice-start
  8.2 1.3 slice-done
  9.5 1.2 pad_maximum_fusion.1
  10.7 148.0 %step.1 = (bf16[2,8,32,3072]{3,2,1,0:T(8,128)(2,1)}, bf16[8,8,3072]{2,1,0:T(8,128)(2,1)}, bf16[4,192,384]{2,1,0:T(8,128)(2,1)}) custom-call(bf16[4,192,384]{2,1,0:T(8,128)(2,1)} %bitcast.48, bf16[256,3072]{1,0:T(8,128)(2,1)} %bitcast.43, bf16[256,3072]{1,0:T(8,128)(2,1)} %bitcast.44, f32[4,3072]{1,0:T(4,128)} %concatenate.21.mods), custom_call_target="tpu_custom_call" | custom-call | tf_op jit(solution)/shard_map/step/pallas_call | solution.py:690
  158.8 0.0 copy-start.2
  158.8 2.2 %slice_bitcast_fusion = (bf16[8,32,3072]{2,1,0:T(8,128)(2,1)S(1)}, bf16[8,32,3072]{2,1,0:T(8,128)(2,1)S(1)}) fusion(bf16[2,8,32,3072]{3,2,1,0:T(8,128)(2,1)} %get-tuple-element.8), kind=kLoop, calls=%fused_computation.4 | loop fusion | bytes 6291456 | tf_op jit(solution)/shard_map/squeeze | solution.py:762
  161.0 0.0 copy-done.2
  161.0 0.9 bitcast_convert_fusion.1
  161.9 0.1 slice_bitcast_fusion.2
  162.0 0.1 slice.41
  162.1 0.1 slice.43
  162.2 1.2 maximum_bitcast_fusion.1
  163.4 0.0 copy-start.1
  163.4 1.2 maximum_bitcast_fusion
  164.7 0.0 copy-done.1
  164.7 0.1 bitcast_convert_fusion
  164.8 0.3 fusion.1
  165.1 1.1 copy.22
  166.2 1.1 copy.21
  (2 shorter events, 0.1 us)
Async XLA Ops:
  0.6 5.2 %copy-start.3 = (bf16[768,192]{0,1:T(8,128)(2,1)S(1)}, bf16[768,192]{0,1:T(8,128)(2,1)}, u32[]{:S(2)}) copy-start(bf16[768,192]{0,1:T(8,128)(2,1)} %param.16) | copy-start | bytes 884740
  0.6 5.2 %copy-start.4 = (bf16[192,768]{1,0:T(8,128)(2,1)S(1)}, bf16[192,768]{1,0:T(8,128)(2,1)}, u32[]{:S(2)}) copy-start(bf16[192,768]{1,0:T(8,128)(2,1)} %param.15) | copy-start | bytes 884740
  4.7 2.3 %copy-start = (bf16[1,192,3072]{2,1,0:T(8,128)(2,1)S(1)}, bf16[1,192,3072]{2,1,0:T(8,128)(2,1)}, u32[]{:S(2)}) copy-start(bf16[1,192,3072]{2,1,0:T(8,128)(2,1)} %param.9) | copy-start | bytes 3538948
  8.2 1.3 slice-start
  158.8 2.2 %copy-start.2 = (bf16[8,8,3072]{2,1,0:T(8,128)(2,1)S(1)}, bf16[8,8,3072]{2,1,0:T(8,128)(2,1)}, u32[]{:S(2)}) copy-start(bf16[8,8,3072]{2,1,0:T(8,128)(2,1)} %get-tuple-element.10) | copy-start | bytes 1179652
  163.4 1.2 copy-start.1
